TPU v7x, 512 devices: a whole 4x8x8 slice. The times are simulated.
512 devices in a mesh: blk: 64 (over y, x, z_lo), ga: 8 (over z_hi, core).
Axes of the slice: x: 4, y: 8, z: 8 (z_hi: 4, z_lo: 2; z = z_hi * 2 + z_lo), core: 2. Of those that a mesh axis runs over, the one named last changes fastest.
Arguments:
- pair_elements: bfloat16 [4096, 65536], P('ga', 'blk'), may hold values from -6 to 6
- screening: bfloat16 [4096, 4096], P('ga', 'blk'), may hold values from -0.09375 to 0.09375
- energies: float32 [1024], replicated, may hold values from 0.5 to 3
- frequencies: float32 [8], replicated, may hold values from 0.3 to 3
- qp_index: int32 [32], replicated, may hold values from 0 to 1023
- occupied: int32 [1024], replicated, may hold values 0 or 1
Outputs:
- self_energy: float32 [2, 8, 32, 32], replicated
All inputs are finite; a program needn't handle non-finite values.
Results may differ from a plain program's by a relative error of at most 0.0003.
Values may be sent and summed in bfloat16 or wider, within the bound.
A program may use at most 64 MiB of HBM per device.

v0:
```python
import jax
import jax.numpy as jnp
from jax import lax
from jax.sharding import Mesh
from jax.sharding import PartitionSpec as P

STATES = 32
NG = 4096
BLK = ("blk_0", "blk_1", "blk_2")
BLK_GA = ("blk_0", "blk_1", "blk_2", "ga")


def laid_out(pieces, dim):
    dims = list(pieces.shape[1:])
    dims[dim] *= pieces.shape[0]
    return jnp.moveaxis(pieces, 0, dim).reshape(dims)


def all_blocks(shard, axes, order):
    pieces = shard[None]
    for k in order:
        pieces = lax.all_gather(pieces, axes[k], axis=0, tiled=True)
    block = [lax.axis_size(axes[k]) for k in reversed(order)]
    pieces = pieces.reshape(*block, *shard.shape)
    turned = sorted(range(len(order)), key=lambda place: order[len(order) - 1 - place])
    return pieces.transpose(*turned, *range(len(order), pieces.ndim)).reshape(-1, *shard.shape)


def gathered_by_axis(shard, axes, order, dim):
    return laid_out(all_blocks(shard, axes, order), dim)


def band_weights(energies, frequencies, qp_index, occupied, offset, band_count):
    level_count = energies.shape[0]
    position = jnp.arange(level_count, dtype=jnp.int32)
    signed = jnp.where(occupied == 1, -energies, energies)
    onehot = (qp_index[:, None] == position[None, :]).astype(jnp.float32)
    state_level = jnp.sum(onehot * signed[None, :], axis=1)
    band_level = lax.dynamic_slice_in_dim(signed, offset, band_count, 0)
    detuning = state_level[:, None] - band_level[None, :]
    imag_freq = frequencies[:, None, None]
    modulus = detuning[None] ** 2 + imag_freq**2
    return (detuning[None] / modulus, -imag_freq / modulus)


def window_sigma(elements, screened, weight_real, weight_imag, band_count):
    row_count = elements.shape[0]
    local_elems = elements.astype(jnp.float32).reshape(row_count, band_count, 2, STATES)
    image_cols = screened.reshape(row_count, band_count, 2, STATES)
    intersection = jnp.einsum(
        "gnpi,gnqj->npiqj", local_elems, image_cols, precision=lax.Precision.HIGHEST
    )
    intersection_real = intersection[:, 0, :, 0, :] + intersection[:, 1, :, 1, :]
    intersection_imag = intersection[:, 0, :, 1, :] - intersection[:, 1, :, 0, :]
    sigma_real = jnp.einsum(
        "kin,nij->kij", weight_real, intersection_real, precision=lax.Precision.HIGHEST
    ) - jnp.einsum("kin,nij->kij", weight_imag, intersection_imag, precision=lax.Precision.HIGHEST)
    sigma_imag = jnp.einsum(
        "kin,nij->kij", weight_real, intersection_imag, precision=lax.Precision.HIGHEST
    ) + jnp.einsum("kin,nij->kij", weight_imag, intersection_real, precision=lax.Precision.HIGHEST)
    return jnp.stack([sigma_real, sigma_imag]) / NG


def shards(pair_elements, screening, energies, frequencies, qp_index, occupied):
    col_count = pair_elements.shape[1]
    band_count = col_count // (2 * STATES)
    gathered = lax.all_gather(pair_elements, "ga", axis=0, tiled=True)
    screened = jnp.dot(
        gathered_by_axis(screening, BLK, (2, 0, 1), 1), gathered, preferred_element_type=jnp.float32
    )
    band_start = lax.axis_index(BLK) * band_count
    weight_real, weight_imag = band_weights(
        energies, frequencies, qp_index, occupied, band_start, band_count
    )
    partial_value = window_sigma(pair_elements, screened, weight_real, weight_imag, band_count)
    return lax.psum(partial_value, BLK_GA)


def solution(mesh):
    torus = Mesh(mesh.devices.reshape(8, 4, 2, mesh.shape["ga"]), ("blk_0", "blk_1", "blk_2", "ga"))
    in_specs = (P("ga", BLK), P("ga", BLK), P(), P(), P(), P())
    out_specs = P()
    return jax.shard_map(
        shards, mesh=torus, in_specs=in_specs, out_specs=out_specs, check_vma=False
    )
```

profile of v0, /device:TPU:1, one launch (start us, length us, event | category | flops | bytes accessed | tf_op | source)
XLA Modules:
  0.0 498.4 jit_solution(6160109027785036022)
XLA Ops:
  6.5 0.0 copy-start.1
  6.5 0.0 copy-start.2
  6.5 0.0 copy-start.3
  6.5 0.0 copy-start.4
  6.5 0.0 all-gather.5.cloned.1.call-start
  6.6 5.5 %all-gather = bf16[1024,64]{0,1:T(8,128)(2,1)S(1)} all-gather(bf16[512,64]{0,1:T(8,128)(2,1)} %param.7), channel_id=2, replica_groups=mesh['blk_0'=8,'blk_1'=4,'blk_2'=2,'ga'=8] {'blk_2'}, dimensions={0}, use_global_device_ids=true | all-gather | bytes 196608 | tf_op jit(solution)/shard_map/all_gather | solution.py:22
  12.1 0.7 copy.75
  12.7 0.0 all-gather.5.cloned.1.call-update
  12.8 0.0 all-gather.7.cloned.1.call-start
  12.8 41.2 %all-gather.5.cloned.1.call-done = bf16[16,512,64]{1,2,0:T(8,128)(2,1)} async-done(((bf16[2,512,64]{1,2,0:T(8,128)(2,1)}), bf16[16,512,64]{1,2,0:T(8,128)(2,1)}) %all-gather.5.cloned.1.call-update) | async-done | bytes 1048592 | tf_op jit(solution)/shard_map/all_gather | solution.py:22
  54.0 0.0 all-gather.7.cloned.1.call-update
  54.0 0.0 all-gather.9.cloned.1.call-start
  54.1 2.3 copy.61
  56.4 0.0 all-gather.9.cloned.1.call-update
  56.4 0.0 all-reduce.2.cloned.1.call-start
  56.4 0.0 copy-done.1
  56.4 0.0 copy-done.2
  56.5 0.1 dynamic_slice.3
  56.5 0.0 copy-done.3
  56.5 0.2 select_reduce_fusion
  56.7 0.0 copy-done.4
  56.8 0.1 broadcast_subtract_fusion
  56.8 56.5 %all-gather.7.cloned.1.call-done = bf16[64,512,64]{1,2,0:T(8,128)(2,1)} async-done(((bf16[16,512,64]{1,2,0:T(8,128)(2,1)}), bf16[64,512,64]{1,2,0:T(8,128)(2,1)}) %all-gather.7.cloned.1.call-update) | async-done | bytes 4194320 | tf_op jit(solution)/shard_map/all_gather | solution.py:22
  113.3 4.6 copy.60
  117.9 84.5 %all-gather.9.cloned.1.call-done = bf16[4096,1024]{0,1:T(8,128)(2,1)} async-done(((bf16[512,1024]{0,1:T(8,128)(2,1)}), bf16[4096,1024]{0,1:T(8,128)(2,1)}) %all-gather.9.cloned.1.call-update) | async-done | bytes 8388624 | tf_op jit(solution)/shard_map/all_gather | solution.py:67
  202.4 0.0 copy-start
  202.4 8.2 %fusion.25 = f32[512,16,2,32]{0,3,2,1:T(8,128)S(1)} fusion(bf16[512,4096,1,1]{0,1,3,2:T(8,128)(2,1)} %bitcast.52, bf16[16,2,32,4096]{3,2,1,0:T(8,128)(2,1)} %bitcast.55), kind=kOutput, calls=%fused_computation.35 | convolution fusion | flops 4294967296 | bytes 14680064 | tf_op jit(solution)/shard_map/dot_general | solution.py:68
  210.6 0.0 copy-done
  210.6 2.7 fusion.2
  213.3 0.1 fusion.8
  213.4 0.2 copy.65
  213.6 0.2 copy.64
  213.7 0.4 fusion.9
  214.2 0.4 fusion.10
  214.6 0.4 fusion.5
  215.0 0.4 fusion.6
  215.4 0.7 maximum_multiply_fusion
  216.2 0.0 all-reduce.2.cloned.1.call-update
  216.2 274.0 %all-reduce.2.cloned.1.call-done = f32[2,8,32,32]{3,1,2,0:T(8,128)} async-done(((f32[2,8,32,32]{3,1,2,0:T(8,128)}), f32[2,8,32,32]{3,1,2,0:T(8,128)}) %all-reduce.2.cloned.1.call-update) | async-done | bytes 65552 | tf_op jit(solution)/shard_map/psum | solution.py:76
  490.2 1.7 copy.68
  (2 shorter events, 0.0 us)
Async XLA Ops:
  6.5 49.9 %copy-start.1 = (f32[1024]{0:T(1024)S(1)}, f32[1024]{0:T(1024)}, u32[]{:S(2)}) copy-start(f32[1024]{0:T(1024)} %param.8) | copy-start | bytes 12292
  6.5 49.9 %copy-start.2 = (s32[1024]{0:T(1024)S(1)}, s32[1024]{0:T(1024)}, u32[]{:S(2)}) copy-start(s32[1024]{0:T(1024)} %param.11) | copy-start | bytes 12292
  6.5 50.0 %copy-start.3 = (s32[32]{0:T(128)S(1)}, s32[32]{0:T(128)}, u32[]{:S(2)}) copy-start(s32[32]{0:T(128)} %param.10) | copy-start | bytes 388
  6.5 50.2 %copy-start.4 = (f32[8]{0:T(128)S(1)}, f32[8]{0:T(128)}, u32[]{:S(2)}) copy-start(f32[8]{0:T(128)} %param.9) | copy-start | bytes 100
  6.5 47.4 %all-gather.5.cloned.1.call-start = ((), (), s32[]{:S(2)}) async-start(), calls=%async_computation | async-start | bytes 1179648 | tf_op jit(solution)/shard_map/all_gather | solution.py:22
  12.8 100.5 %all-gather.7.cloned.1.call-start = ((), (), s32[]{:S(2)}) async-start(), calls=%async_computation.1 | async-start | bytes 5242880 | tf_op jit(solution)/shard_map/all_gather | solution.py:22
  54.0 148.4 %all-gather.9.cloned.1.call-start = ((), (), s32[]{:S(2)}) async-start(), calls=%async_computation.2 | async-start | bytes 9437184 | tf_op jit(solution)/shard_map/all_gather | solution.py:67
  56.4 433.8 %all-reduce.2.cloned.1.call-start = ((), (), s32[]{:S(2)}) async-start(), calls=%async_computation.3 | async-start | bytes 524288 | tf_op jit(solution)/shard_map/psum | solution.py:76
  202.4 8.2 %copy-start = (bf16[512,1024]{0,1:T(8,128)(2,1)S(1)}, bf16[512,1024]{0,1:T(8,128)(2,1)}, u32[]{:S(2)}) copy-start(bf16[512,1024]{0,1:T(8,128)(2,1)} %copy.61) | copy-start | bytes 3145732
Sparse Core Ops, SparseCore 0:
  12.9 41.0 all-gather.4
  56.1 57.1 all-gather.6
  115.4 86.9 all-gather.8
  216.3 273.8 all-reduce.1
where the time goes:
time: 499 us; the launch traced here: 498 us
  waiting for transfers between devices  456 us (91%)
  between operations  13.3 us (3%)
  matrix products  12.6 us (3%)
  local copies, waits for them, and re-layouts  9.7 us (2%)
  blocking collectives  5.5 us (1%)
    psum x1, waiting for transfers between devices, shards(): return lax.psum(partial_value, BLK_GA)  274 us
    all_gather x2, waiting for transfers between devices, all_blocks(): pieces = lax.all_gather(pieces, axes[k], axis=0, tiled=True)  97.6 us
    all_gather x1, waiting for transfers between devices, shards(): gathered = lax.all_gather(pair_elements, 'ga', axis=0, tiled=True)  84.5 us
  transfers between devices with their start and end apart: 4, of which 4 were waited for; matrix products, arithmetic and copies ran while one was open for 1% of the time, Pallas kernels for 0%

commit v1 on v0

v1 whole, which is shorter than its diff:
```python
import functools

import jax
import jax.numpy as jnp
from jax import lax
from jax.experimental import pallas as pl
from jax.experimental.pallas import tpu as pltpu
from jax.sharding import Mesh
from jax.sharding import PartitionSpec as P

STATES = 32
NG = 4096
NX, NY, NH = 4, 8, 4
ROWS = 512
COLS = 1024
BANDS = 16
BLK = ("y", "x", "zl")
GA = ("zh", "core")
MESH = pl.DeviceIdType.MESH
BF16, F32 = jnp.bfloat16, jnp.float32
PIECES = 4
PROWS = ROWS // PIECES


def kernel(
    m_ref, wt_ref, energy, freq, qp, occ, out_ref,
    mbuf, wown, wraw, slab, mt0, mt1, t1, t2, weight, sig, part, gath1, gath2, gath3, final,
    m_local, w_local, m_send, m_recv, f_send, f_recv, w_send, w_recv,
    ax_s, ax_r, ay_s, ay_r, by_s, by_r, bx_s, bx_r, r_send, r_recv,
):
    y, x = lax.axis_index("y"), lax.axis_index("x")
    zl, zh, k = lax.axis_index("zl"), lax.axis_index("zh"), lax.axis_index("core")
    other = 1 - k

    def up(v, d, n):
        return lax.rem(v + (d + n), n)

    def local(src, dst, sem):
        return pltpu.make_async_copy(src, dst, sem)

    def remote(src, dst, send, recv, **where):
        return pltpu.make_async_remote_copy(
            src_ref=src, dst_ref=dst, send_sem=send, recv_sem=recv,
            device_id=where, device_id_type=MESH,
        )

    own_m = local(m_ref, mbuf.at[0, k], m_local)
    own_m.start()
    own_w = local(wt_ref, wown, w_local.at[0])
    own_w.start()

    barrier = pltpu.get_barrier_semaphore()
    peers = []
    for step in range(1, 8):
        peers.append({"x": lax.rem(x + step // 2, NX), "core": lax.rem(k + step % 2, 2)})
        peers.append({"y": lax.rem(y + step, NY)})
        peers.append({"zh": lax.rem(zh + step // 2, NH), "zl": lax.rem(zl + step % 2, 2)})
    down_y, down_h = up(y, -2, NY), up(zh, -1, NH)
    over_y, over_h = up(y, 2, NY), up(zh, 1, NH)
    for side in range(2):
        peers.append({"y": down_y, "zh": down_h, "zl": jnp.int32(side)})
        peers.append({"y": over_y, "zh": over_h, "zl": jnp.int32(side)})
    for peer in peers:
        pl.semaphore_signal(barrier, inc=1, device_id=peer, device_id_type=MESH)

    def level(at):
        return jnp.where(occ[at] == 1, -energy[at], energy[at])

    sub = lax.broadcasted_iota(jnp.int32, (STATES, 128), 0)
    lane_freq = lax.broadcasted_iota(jnp.int32, (STATES, 128), 1) // STATES
    state = jnp.zeros((STATES, 128), F32)
    for i in range(STATES):
        state = jnp.where(sub == i, level(qp[i]), state)
    window = []
    for half in range(2):
        row = jnp.zeros((STATES, 128), F32)
        for j in range(4):
            row = jnp.where(lane_freq == j, freq[4 * half + j], row)
        window.append(row)
    band0 = ((y * NX + x) * 2 + zl) * BANDS

    @pl.loop(0, BANDS)
    def _(n):
        gap = state - level(band0 + n)
        for half in range(2):
            modulus = gap * gap + window[half] * window[half]
            weight[n, half, 0] = gap / modulus
            weight[n, half, 1] = -window[half] / modulus

    own_w.wait()
    pl.semaphore_wait(barrier, len(peers))

    special = (y // 2) == lax.rem(zh + 2, NH)

    @pl.when(jnp.logical_not(special))
    def _():
        remote(wown, wraw.at[zl], w_send.at[0], w_recv.at[zl], zl=1 - zl).start()
        local(wt_ref, wraw.at[zl], w_local.at[1]).start()

    @pl.when(special)
    def _():
        for side in range(2):
            remote(
                wown, wraw.at[zl], w_send.at[side], w_recv.at[zl],
                y=down_y, zh=down_h, zl=jnp.int32(side),
            ).start()

    own_m.wait()

    def m_rows(p):
        return pl.ds(p * PROWS, PROWS)

    def m_copy(p, way):
        src = mbuf.at[0, k, m_rows(p)]
        if way == 0:
            return remote(
                src, mbuf.at[2, k, m_rows(p)], m_send.at[0, p], m_recv.at[0, p], zh=up(zh, 1, NH)
            )
        if way == 1:
            return remote(
                src, mbuf.at[1, k, m_rows(p)], m_send.at[1, p], m_recv.at[1, p], zh=up(zh, -1, NH)
            )
        return remote(
            src, mbuf.at[0, k, m_rows(p)], m_send.at[2, p], m_recv.at[2, p], core=other
        )

    for p in range(PIECES):
        for way in range(2):
            m_copy(p, way).start()
    for p in range(PIECES):
        m_copy(p, 2).start()

    def m_landed(p, way):
        m_copy(p, way).wait_recv()

    def forward(p, way):
        place = mbuf.at[2 - way, k, m_rows(p)]
        return remote(place, place, f_send.at[way, p], f_recv.at[way, p], core=other)

    def pass_on(p):
        for way in range(2):
            m_landed(p, way)
            forward(p, way).start()

    @pl.when(jnp.logical_not(special))
    def _():
        remote(wown, wraw.at[1 - zl], w_send.at[0], w_recv.at[1 - zl], zl=1 - zl).wait_recv()
        local(wt_ref, wraw.at[zl], w_local.at[1]).wait()

    @pl.when(special)
    def _():
        for side in range(2):
            remote(
                wown, wraw.at[side], w_send.at[side], w_recv.at[side],
                y=down_y, zh=down_h, zl=jnp.int32(side),
            ).wait_recv()

    slab[y, x] = jnp.concatenate([wraw[0], wraw[1]], axis=0).T

    sign = (1, -1)

    def quarter(kind, h):
        return pl.ds((2 * kind + h) * 128, 128)

    def ax(h, i):
        s = sign[h]
        src = x if i < 2 else up(x, -s, NX)
        place = slab.at[y, src, quarter(0, h)]
        return remote(place, place, ax_s.at[h, i], ax_r.at[h, i], x=up(x, -s if i == 1 else s, NX))

    def ring_y(h, i):
        s = sign[h]
        if i < 4:
            return up(y, -s * i, NY), up(y, s, NY)
        return up(y, s * (i - 4), NY), up(y, -s, NY)

    def ay(h, i):
        src, to = ring_y(h, i)
        place = slab.at[src, :, quarter(0, h)]
        return remote(place, place, ay_s.at[h, i], ay_r.at[h, i], y=to)

    def by(h, i):
        src, to = ring_y(h, i)
        place = slab.at[src, x, quarter(1, h)]
        return remote(place, place, by_s.at[h, i], by_r.at[h, i], y=to)

    def bx(h, i):
        s = sign[h]
        src = x if i < 2 else up(x, -s, NX)
        place = slab.at[:, src, quarter(1, h)]
        return remote(place, place, bx_s.at[h, i], bx_r.at[h, i], x=up(x, -s if i == 1 else s, NX))

    def go(copy, *at):
        for h in range(2):
            for i in at:
                copy(h, i).start()

    def step(copy, *pairs):
        for h in range(2):
            for got, then in pairs:
                copy(h, got).wait_recv()
                if then is not None:
                    copy(h, then).start()

    go(by, 0, 4)
    go(ax, 0, 1)
    mt0[...] = mbuf[0, k].T
    step(ax, (0, 2))
    step(by, (0, 1), (4, 5))
    step(ax, (1, None), (2, None))
    go(ay, 0, 4)
    step(by, (1, 2), (5, 6))
    step(by, (2, 3), (6, None))
    step(ay, (0, 1), (4, 5))
    step(by, (3, None))
    go(bx, 0, 1)
    pass_on(0)
    step(ay, (1, 2), (5, 6))
    step(bx, (0, 2))
    pass_on(1)
    step(ay, (2, 3), (6, None))
    step(bx, (1, None), (2, None))
    step(ay, (3, None))
    pass_on(2)
    for p in range(PIECES):
        m_landed(p, 2)
    for p in range(PIECES - 1):
        for way in range(2):
            forward(p, way).wait_recv()

    chunk_of = (zh, up(zh, 1, NH), up(zh, -1, NH), up(zh, 2, NH))

    def w_block(chunk, p):
        base = 2 * chunk_of[chunk]
        return [slab[base, p], slab[base + 1, p]]

    def m_block(j, p, columns):
        return [mbuf[j, 0, m_rows(p), columns], mbuf[j, 1, m_rows(p), columns]]

    def multiply(terms, columns):
        left, right = [], []
        for chunk, j, p in terms:
            left += w_block(chunk, p)
            right += m_block(j, p, columns)
        return jnp.dot(
            jnp.concatenate(left, axis=1), jnp.concatenate(right, axis=0),
            preferred_element_type=F32,
        )

    early = [p for p in range(PIECES - 1)]
    last = PIECES - 1

    for p in early:
        mt1[:, pl.ds(p * PROWS, PROWS)] = mbuf[1, k, m_rows(p)].T

    @pl.loop(0, 4)
    def _(g):
        columns = pl.ds(pl.multiple_of(g * 256, 256), 256)
        own = [(0, 0, p) for p in range(PIECES)]
        t1[:, columns] = multiply(
            own + [(1, 1, p) for p in early] + [(2, 2, p) for p in early], columns
        )
        t2[:, columns] = multiply([(3, 2, p) for p in early], columns)

    pass_on(last)
    mt1[:, pl.ds(last * PROWS, PROWS)] = mbuf[1, k, m_rows(last)].T
    for way in range(2):
        forward(last, way).wait_recv()

    def split(value):
        high = value.astype(BF16)
        return [high, (value - high.astype(F32)).astype(BF16)]

    sig[...] = jnp.zeros_like(sig)

    @pl.loop(0, 4)
    def _(g):
        columns = pl.ds(pl.multiple_of(g * 256, 256), 256)
        first = t1[:, columns] + multiply([(1, 1, last), (2, 2, last)], columns)
        second = t2[:, columns] + multiply([(3, 2, last)], columns)
        left0, left1 = mt0[columns, :], mt1[columns, :]
        part[...] = jnp.dot(
            jnp.concatenate([left0, left0, left1, left1], axis=1),
            jnp.concatenate(split(first) + split(second), axis=0),
            preferred_element_type=F32,
        )
        sums = [sig[pl.ds(STATES * v, STATES), :] for v in range(4)]
        for b in range(4):
            block = part[pl.ds(64 * b, 64), :][:, 64 * b : 64 * b + 64]
            real = block[:STATES, :STATES] + block[STATES:, STATES:]
            imag = block[:STATES, STATES:] - block[STATES:, :STATES]
            real = jnp.concatenate([real] * 4, axis=1)
            imag = jnp.concatenate([imag] * 4, axis=1)
            for half in range(2):
                w_real = weight[4 * g + b, half, 0]
                w_imag = weight[4 * g + b, half, 1]
                sums[half] += w_real * real - w_imag * imag
                sums[2 + half] += w_real * imag + w_imag * real
        for v in range(4):
            sig[pl.ds(STATES * v, STATES), :] = sums[v]

    slot = 2 * x + k

    def every(phase, buffer):
        block = buffer.at[pl.ds(0, 7)]
        local(block, block, r_recv.at[phase]).wait()

    def drained(phase, buffer):
        block = buffer.at[pl.ds(0, 7)]
        local(block, block, r_send.at[phase]).wait()

    def total(buffer):
        value = buffer[0]
        for i in range(1, 8):
            value = value + buffer[i]
        return value

    def rows_of(i):
        return pl.ds(pl.multiple_of(i * 16, 16), 16)

    for hop in range(1, 8):
        to_x, to_k = lax.rem(x + hop // 2, NX), lax.rem(k + hop % 2, 2)
        remote(
            sig.at[rows_of(2 * to_x + to_k)], gath1.at[slot], r_send.at[0], r_recv.at[0],
            x=to_x, core=to_k,
        ).start()
    gath1[slot] = sig[rows_of(slot), :]
    every(0, gath1)
    gath2[y] = total(gath1)
    for hop in range(1, 8):
        remote(
            gath2.at[y], gath2.at[y], r_send.at[1], r_recv.at[1], y=lax.rem(y + hop, NY)
        ).start()
    every(1, gath2)
    place = 2 * zh + zl
    gath3[place] = total(gath2)
    for hop in range(1, 8):
        remote(
            gath3.at[place], gath3.at[place], r_send.at[2], r_recv.at[2],
            zh=lax.rem(zh + hop // 2, NH), zl=lax.rem(zl + hop % 2, 2),
        ).start()
    every(2, gath3)
    final[slot] = total(gath3) * (1.0 / NG)
    for hop in range(1, 8):
        remote(
            final.at[slot], final.at[slot], r_send.at[3], r_recv.at[3],
            x=lax.rem(x + hop // 2, NX), core=lax.rem(k + hop % 2, 2),
        ).start()
    every(3, final)
    for i in range(8):
        out_ref[pl.ds(16 * i, 16), :] = final[i]

    for p in range(PIECES):
        for way in range(3):
            m_copy(p, way).wait_send()
        for way in range(2):
            forward(p, way).wait_send()
    for h in range(2):
        for i in range(3):
            ax(h, i).wait_send()
            bx(h, i).wait_send()
        for i in range(7):
            ay(h, i).wait_send()
            by(h, i).wait_send()
    remote(wown, wraw.at[zl], w_send.at[0], w_recv.at[zl], zl=1 - zl).wait_send()

    @pl.when(special)
    def _():
        remote(wown, wraw.at[zl], w_send.at[1], w_recv.at[zl], zl=1 - zl).wait_send()

    drained(0, gath1)
    drained(1, gath2)
    drained(2, gath3)
    drained(3, final)


def shards(pair_elements, screening, energies, frequencies, qp_index, occupied):
    vmem = functools.partial(pltpu.VMEM)
    dma = pltpu.SemaphoreType.DMA
    smem = pl.BlockSpec(memory_space=pltpu.SMEM)
    anywhere = pl.BlockSpec(memory_space=pl.ANY)
    packed = pl.pallas_call(
        kernel,
        out_shape=jax.ShapeDtypeStruct((128, 128), F32),
        in_specs=[anywhere, anywhere, smem, smem, smem, smem],
        out_specs=pl.BlockSpec(memory_space=pltpu.VMEM),
        scratch_shapes=[
            vmem((3, 2, ROWS, COLS), BF16),
            vmem((64, ROWS), BF16),
            vmem((2, 64, ROWS), BF16),
            vmem((NY, NX, ROWS, 128), BF16),
            vmem((COLS, ROWS), BF16),
            vmem((COLS, ROWS), BF16),
            vmem((ROWS, COLS), F32),
            vmem((ROWS, COLS), F32),
            vmem((BANDS, 2, 2, STATES, 128), F32),
            vmem((128, 128), F32),
            vmem((256, 256), F32),
            vmem((8, 16, 128), F32),
            vmem((8, 16, 128), F32),
            vmem((8, 16, 128), F32),
            vmem((8, 16, 128), F32),
            dma,
            dma((2,)),
            dma((3, PIECES)),
            dma((3, PIECES)),
            dma((2, PIECES)),
            dma((2, PIECES)),
            dma((2,)),
            dma((2,)),
            dma((2, 3)),
            dma((2, 3)),
            dma((2, 7)),
            dma((2, 7)),
            dma((2, 7)),
            dma((2, 7)),
            dma((2, 3)),
            dma((2, 3)),
            dma((4,)),
            dma((4,)),
        ],
        compiler_params=pltpu.CompilerParams(collective_id=0, has_side_effects=True),
    )(pair_elements, screening.T, energies, frequencies, qp_index, occupied)
    packed = packed.reshape(2, 2, STATES, 4, STATES)
    return packed.transpose(0, 1, 3, 2, 4).reshape(2, 8, STATES, STATES)


def solution(mesh):
    torus = Mesh(mesh.devices.reshape(NY, NX, 2, NH, 2), ("y", "x", "zl", "zh", "core"))
    in_specs = (P(GA, BLK), P(GA, BLK), P(), P(), P(), P())
    return jax.shard_map(
        shards, mesh=torus, in_specs=in_specs, out_specs=P(), check_vma=False
    )
```

time: 499 us -> 111 us (0.22)
  waiting for transfers between devices: 456 us -> 0 us
  Pallas kernels: 0 us -> 109 us
  between operations: 13.3 us -> 0.02 us
  matrix products: 12.6 us -> 0 us
  local copies, waits for them, and re-layouts: 9.7 us -> 1.73 us
  blocking collectives: 5.5 us -> 0 us
    psum x1 -> x0, waiting for transfers between devices: 274 us -> none  [shards(): return lax.psum(partial_value, BLK_GA)]
    all_gather x3 -> x0, waiting for transfers between devices: 182 us -> none  [the longest x2 97.6 us: all_blocks(): pieces = lax.all_gather(pieces, axes[k], axis=0, tiled=True)]
    pallas_call x0 -> x1, Pallas kernels: none -> 109 us  [shards(): pl.pallas_call(kernel, out_shape=jax.ShapeDtypeStruct((128, 128), F32), i...]
    dot_general x6 -> x0, matrix products: 12.6 us -> none  [the longest x1 8.22 us: shards(): jnp.dot(gathered_by_axis(screening, BLK, (2, 0, 1), 1), gathered, preferr...]
    all_gather x1 -> x0, blocking collectives: 5.5 us -> none  [all_blocks(): pieces = lax.all_gather(pieces, axes[k], axis=0, tiled=True)]
  transfers between devices with their start and end apart: 4 -> 0, of which waited for: 4 -> 0; matrix products, arithmetic and copies ran while one was open for 1% -> 0% of each run, Pallas kernels for 0% -> 0%
where the time goes in v1:
time: 111 us
  Pallas kernels  109 us (98%)
  local copies, waits for them, and re-layouts  1.73 us (2%)
    pallas_call x1, Pallas kernels, shards(): pl.pallas_call(kernel, out_shape=jax.ShapeDtypeStruct((128, 128), F32), i...  109 us

profile of v1, /device:TPU:1, one launch (start us, length us, event | category | flops | bytes accessed | tf_op | source)
XLA Modules:
  0.0 111.2 jit_solution(17300712056084791525)
XLA Ops:
  0.0 109.5 %shard_map.64 = f32[128,128]{1,0:T(8,128)} custom-call(bf16[512,1024]{1,0:T(8,128)(2,1)} %m_ref.1, bf16[64,512]{1,0:T(8,128)(2,1)} %bitcast.4, f32[1024]{0:T(1024)} %energy.1, f32[8]{0:T(128)} %freq.1, s32[32]{0:T(128)} %qp.1, s32[1024]{0:T(1024)} %occ.1), custom_call_target="tpu_custom_call" | custom-call | tf_op jit(solution)/shard_map/pallas_call | solution.py:382
  109.5 1.0 reshape.6
  110.5 0.7 copy.7

commit v2 on v1

--- a/solution.py
+++ b/solution.py
@@ -105,8 +105,6 @@
                 y=down_y, zh=down_h, zl=jnp.int32(side),
             ).start()
 
-    own_m.wait()
-
     def m_rows(p):
         return pl.ds(p * PROWS, PROWS)
 
@@ -124,12 +122,6 @@
             src, mbuf.at[0, k, m_rows(p)], m_send.at[2, p], m_recv.at[2, p], core=other
         )
 
-    for p in range(PIECES):
-        for way in range(2):
-            m_copy(p, way).start()
-    for p in range(PIECES):
-        m_copy(p, 2).start()
-
     def m_landed(p, way):
         m_copy(p, way).wait_recv()
 
@@ -155,6 +147,10 @@
                 y=down_y, zh=down_h, zl=jnp.int32(side),
             ).wait_recv()
 
+    own_m.wait()
+    for p in range(PIECES):
+        for way in range(2):
+            m_copy(p, way).start()
     slab[y, x] = jnp.concatenate([wraw[0], wraw[1]], axis=0).T
 
     sign = (1, -1)
@@ -204,6 +200,8 @@
 
     go(by, 0, 4)
     go(ax, 0, 1)
+    for p in range(PIECES):
+        m_copy(p, 2).start()
     mt0[...] = mbuf[0, k].T
     step(ax, (0, 2))
     step(by, (0, 1), (4, 5))
@@ -214,16 +212,15 @@
     step(ay, (0, 1), (4, 5))
     step(by, (3, None))
     go(bx, 0, 1)
-    pass_on(0)
     step(ay, (1, 2), (5, 6))
     step(bx, (0, 2))
-    pass_on(1)
     step(ay, (2, 3), (6, None))
     step(bx, (1, None), (2, None))
     step(ay, (3, None))
-    pass_on(2)
     for p in range(PIECES):
         m_landed(p, 2)
+    for p in range(PIECES - 1):
+        pass_on(p)
     for p in range(PIECES - 1):
         for way in range(2):
             forward(p, way).wait_recv()
@@ -326,29 +323,47 @@
         ).start()
     gath1[slot] = sig[rows_of(slot), :]
     every(0, gath1)
-    gath2[y] = total(gath1)
+    place = 2 * zh + zl
+    chip = total(gath1)
+    gath2[0, y] = chip[:8]
+    gath2[1, place] = chip[8:]
+
+    def to_y(hop):
+        return {"y": lax.rem(y + hop, NY)}
+
+    def to_z(hop):
+        return {"zh": lax.rem(zh + hop // 2, NH), "zl": lax.rem(zl + hop % 2, 2)}
+
+    def spread(buffer, phase, way, at, to):
+        for hop in range(1, 8):
+            remote(
+                buffer.at[way, at], buffer.at[way, at], r_send.at[phase], r_recv.at[phase],
+                **to(hop),
+            ).start()
+
+    spread(gath2, 1, 0, y, to_y)
+    spread(gath2, 2, 1, place, to_z)
+    every(1, gath2.at[0])
+    gath3[0, place] = total(gath2.at[0])
+    spread(gath3, 3, 0, place, to_z)
+    every(2, gath2.at[1])
+    gath3[1, y] = total(gath2.at[1])
+    spread(gath3, 4, 1, y, to_y)
+    every(3, gath3.at[0])
+    every(4, gath3.at[1])
+    final[slot] = jnp.concatenate(
+        [total(gath3.at[0]), total(gath3.at[1])], axis=0
+    ) * (1.0 / NG)
     for hop in range(1, 8):
         remote(
-            gath2.at[y], gath2.at[y], r_send.at[1], r_recv.at[1], y=lax.rem(y + hop, NY)
-        ).start()
-    every(1, gath2)
-    place = 2 * zh + zl
-    gath3[place] = total(gath2)
-    for hop in range(1, 8):
-        remote(
-            gath3.at[place], gath3.at[place], r_send.at[2], r_recv.at[2],
-            zh=lax.rem(zh + hop // 2, NH), zl=lax.rem(zl + hop % 2, 2),
-        ).start()
-    every(2, gath3)
-    final[slot] = total(gath3) * (1.0 / NG)
-    for hop in range(1, 8):
-        remote(
-            final.at[slot], final.at[slot], r_send.at[3], r_recv.at[3],
+            final.at[slot], final.at[slot], r_send.at[5], r_recv.at[5],
             x=lax.rem(x + hop // 2, NX), core=lax.rem(k + hop % 2, 2),
         ).start()
-    every(3, final)
-    for i in range(8):
-        out_ref[pl.ds(16 * i, 16), :] = final[i]
+    every(5, final)
+    for v in range(4):
+        block = jnp.concatenate([final[2 * v], final[2 * v + 1]], axis=0)
+        for j in range(4):
+            out_ref[v // 2, 4 * (v % 2) + j] = block[:, STATES * j : STATES * (j + 1)]
 
     for p in range(PIECES):
         for way in range(3):
@@ -369,9 +384,11 @@
         remote(wown, wraw.at[zl], w_send.at[1], w_recv.at[zl], zl=1 - zl).wait_send()
 
     drained(0, gath1)
-    drained(1, gath2)
-    drained(2, gath3)
-    drained(3, final)
+    drained(1, gath2.at[0])
+    drained(2, gath2.at[1])
+    drained(3, gath3.at[0])
+    drained(4, gath3.at[1])
+    drained(5, final)
 
 
 def shards(pair_elements, screening, energies, frequencies, qp_index, occupied):
@@ -379,9 +396,9 @@
     dma = pltpu.SemaphoreType.DMA
     smem = pl.BlockSpec(memory_space=pltpu.SMEM)
     anywhere = pl.BlockSpec(memory_space=pl.ANY)
-    packed = pl.pallas_call(
+    return pl.pallas_call(
         kernel,
-        out_shape=jax.ShapeDtypeStruct((128, 128), F32),
+        out_shape=jax.ShapeDtypeStruct((2, 8, STATES, STATES), F32),
         in_specs=[anywhere, anywhere, smem, smem, smem, smem],
         out_specs=pl.BlockSpec(memory_space=pltpu.VMEM),
         scratch_shapes=[
@@ -397,8 +414,8 @@
             vmem((128, 128), F32),
             vmem((256, 256), F32),
             vmem((8, 16, 128), F32),
-            vmem((8, 16, 128), F32),
-            vmem((8, 16, 128), F32),
+            vmem((2, 8, 8, 128), F32),
+            vmem((2, 8, 8, 128), F32),
             vmem((8, 16, 128), F32),
             dma,
             dma((2,)),
@@ -416,13 +433,11 @@
             dma((2, 7)),
             dma((2, 3)),
             dma((2, 3)),
-            dma((4,)),
-            dma((4,)),
+            dma((6,)),
+            dma((6,)),
         ],
         compiler_params=pltpu.CompilerParams(collective_id=0, has_side_effects=True),
     )(pair_elements, screening.T, energies, frequencies, qp_index, occupied)
-    packed = packed.reshape(2, 2, STATES, 4, STATES)
-    return packed.transpose(0, 1, 3, 2, 4).reshape(2, 8, STATES, STATES)
 
 
 def solution(mesh):

time: 111 us -> 101 us (0.910)
  Pallas kernels: 109 us -> 99 us
    pallas_call x1, Pallas kernels: 109 us -> 99 us  [shards(): pl.pallas_call(kernel, out_shape=jax.ShapeDtypeStruct((2, 8, STATES, STAT...]
    unnamed x0 -> x1, local copies, waits for them, and re-layouts: none -> 1.67 us
where the time goes in v2:
time: 101 us
  Pallas kernels  99 us (98%)
  local copies, waits for them, and re-layouts  1.67 us (2%)
    pallas_call x1, Pallas kernels, shards(): pl.pallas_call(kernel, out_shape=jax.ShapeDtypeStruct((2, 8, STATES, STAT...  99 us

profile of v2, /device:TPU:1, one launch (start us, length us, event | category | flops | bytes accessed | tf_op | source)
XLA Modules:
  0.0 100.6 jit_solution(15539630644879861776)
XLA Ops:
  0.0 99.0 %shard_map.64 = f32[2,8,32,32]{3,2,1,0:T(8,128)} custom-call(bf16[512,1024]{1,0:T(8,128)(2,1)} %m_ref.1, bf16[64,512]{1,0:T(8,128)(2,1)} %bitcast.1, f32[1024]{0:T(1024)} %energy.1, f32[8]{0:T(128)} %freq.1, s32[32]{0:T(128)} %qp.1, s32[1024]{0:T(1024)} %occ.1), custom_call_target="tpu_custom_call" | custom-call | tf_op jit(solution)/shard_map/pallas_call | solution.py:399
  99.0 1.7 %copy.8 = f32[2,8,32,32]{3,2,1,0:T(8,128)} copy(f32[2,8,32,32]{3,2,1,0:T(8,128)} %shard_map.64) | data formatting | bytes 131072
